TPU v7x, 32 devices: a whole 2x2x4 slice. The times are simulated.
32 devices in a mesh: grp: 4 (over x, core), dev: 8 (over z, y).
Axes of the slice: x: 2, y: 2, z: 4, core: 2. Of those that a mesh axis runs over, the one named last changes fastest.
Arguments:
- layer_input: bfloat16 [65536, 1024], P(('grp', 'dev')), may hold values from -6 to 6
- hidden_pre: bfloat16 [65536, 1024], P(('grp', 'dev')), may hold values from -6 to 6
- out_grad: bfloat16 [65536, 512], P(('grp', 'dev')), may hold values from -6 to 6
- second_weight: bfloat16 [1024, 512], replicated, may hold values from -0.25 to 0.25
- row_grads: bfloat16 [16384, 128], P(('grp', 'dev')), may hold values from -6 to 6
- row_ids: int32 [16384], P(('grp', 'dev')), may hold values from 0 to 2047
- block_counts: int32 [256], P(('grp', 'dev')), may hold values from 1 to 64, as said below
- emb_table: float32 [16384, 128], P('dev'), may hold values from -4 to 4
- adagrad_state: float32 [16384, 128], P('dev'), may hold values from 0.01 to 1
Outputs:
- grad_first: float32 [1024, 1024], P(('grp', 'dev'))
- grad_second: float32 [1024, 512], P(('grp', 'dev'))
- new_table: float32 [16384, 128], P('dev')
- new_state: float32 [16384, 128], P('dev')
Inputs may be any that keep to these rules, and one draw needn't show every extreme that they name: `block_counts`: the used slots of a block are its first ones. In every draw some owner receives full blocks of 64 used slots from every device. `row_ids`: only used slots are read.
All inputs are finite; a program needn't handle non-finite values.
Results may differ from a plain program's by a relative error of at most 0.0029.
Values may be sent and summed in bfloat16 or wider, within the bound.
A program may use at most 128 MiB of HBM per device.

v0:
```python
import jax
import jax.numpy as jnp
from jax import lax
from jax.sharding import PartitionSpec as P

learn_rate = 0.5
epsilon = 1e-08


def segment_rows(gathered, targets, owned):
    height = 512

    def one_block(index):
        wanted = index * height + jnp.arange(height, dtype=jnp.int32)
        onehot = (wanted[:, None] == targets[None, :]).astype(jnp.bfloat16)
        return jnp.dot(onehot, gathered, preferred_element_type=jnp.float32)

    result = lax.map(one_block, jnp.arange(owned // height, dtype=jnp.int32))
    return result.reshape(owned, gathered.shape[1])


def on_device(
    layer_input,
    hidden_pre,
    out_grad,
    second_weight,
    row_grads,
    row_ids,
    block_counts,
    emb_table,
    adagrad_state,
):
    active = jnp.maximum(hidden_pre, jnp.zeros_like(hidden_pre))
    back = jnp.dot(out_grad, second_weight.T, preferred_element_type=jnp.float32)
    d_hidden = (back * (hidden_pre > 0).astype(jnp.float32)).astype(jnp.bfloat16)
    contract = (((0,), (0,)), ((), ()))
    owners = lax.axis_size("dev")
    capacity = row_grads.shape[0] // owners
    usable = (jnp.arange(capacity, dtype=jnp.int32)[None, :] < block_counts[:, None]).reshape(-1)
    sent_ids = jnp.where(usable, row_ids, -1)
    got_grads, got_ids = (
        lax.all_to_all(row_grads, "dev", split_axis=0, concat_axis=0, tiled=True),
        lax.all_to_all(sent_ids, "dev", split_axis=0, concat_axis=0, tiled=True),
    )
    columns = layer_input
    first_share = lax.psum_scatter(
        lax.dot_general(columns, d_hidden, contract, preferred_element_type=jnp.float32),
        "grp",
        scatter_dimension=0,
        tiled=True,
    )
    grad_first = lax.psum_scatter(first_share, "dev", scatter_dimension=0, tiled=True)
    columns = active
    second_share = lax.psum_scatter(
        lax.dot_general(columns, out_grad, contract, preferred_element_type=jnp.float32),
        "grp",
        scatter_dimension=0,
        tiled=True,
    )
    grad_second = lax.psum_scatter(second_share, "dev", scatter_dimension=0, tiled=True)
    owned = emb_table.shape[0]
    local_grad = segment_rows(got_grads, got_ids, owned)
    table_grad = lax.psum(local_grad, "grp")
    new_state = adagrad_state + table_grad * table_grad
    new_table = emb_table - learn_rate * table_grad / (jnp.sqrt(new_state) + epsilon)
    return (grad_first, grad_second, new_table, new_state)


def solution(mesh):
    in_specs = (
        P(("grp", "dev"), None),
        P(("grp", "dev"), None),
        P(("grp", "dev"), None),
        P(),
        P(("grp", "dev"), None),
        P(("grp", "dev")),
        P(("grp", "dev")),
        P("dev", None),
        P("dev", None),
    )
    out_specs = (P(("grp", "dev"), None), P(("grp", "dev"), None), P("dev", None), P("dev", None))
    return jax.shard_map(
        on_device, mesh=mesh, in_specs=in_specs, out_specs=out_specs, check_vma=False
    )
```

profile of v0, /device:TPU:0, one launch (start us, length us, event | category | flops | bytes accessed | tf_op | source)
XLA Modules:
  0.0 275.4 jit_solution(10970960093291804057)
XLA Ops:
  7.2 1.5 copy-done
  8.8 5.9 %fusion.5 = f32[1024,512]{1,0:T(8,128)} fusion(bf16[2048,512]{1,0:T(8,128)(2,1)S(1)} %copy-done, bf16[2048,1024]{1,0:T(8,128)(2,1)} %param.12), kind=kOutput, calls=%fused_computation.8 | convolution fusion | flops 2149580800 | bytes 8388608 | tf_op jit(solution)/shard_map/dot_general | solution.py:55
  14.7 12.3 %fusion.8 = f32[1024,1024]{0,1:T(8,128)} fusion(bf16[2048,1024]{1,0:T(8,128)(2,1)} %param.11, bf16[2048,1024]{1,0:T(8,128)(2,1)} %param.12, bf16[2048,512]{1,0:T(8,128)(2,1)S(1)} %copy-done, bf16[1024,512]{1,0:T(8,128)(2,1)S(1)} %copy-done.3), kind=kOutput, calls=%fused_computation.11 | convolution fusion | flops 6448742400 | bytes 15728640 | tf_op jit(solution)/shard_map/dot_general | solution.py:47
  27.1 0.6 copy-done.4
  27.9 13.7 %all_to_all.24 = s32[8,64,1]{1,2,0:T(1,128)S(1)} all-to-all(s32[8,64,1]{1,2,0:T(1,128)S(1)} %bitcast.26), channel_id=1, replica_groups=mesh['grp'=4,'dev'=8] {'dev'}, dimensions={0} | all-to-all | bytes 4096 | tf_op jit(solution)/shard_map/all_to_all | solution.py:43
  41.7 3.4 %all-to-all-start.1 = ((bf16[8,64,128]{2,1,0:T(8,128)(2,1)}), bf16[8,64,128]{2,1,0:T(8,128)(2,1)S(1)}, u32[]{:S(2)}, u32[]{:S(2)}) async-start(bf16[8,64,128]{2,1,0:T(8,128)(2,1)} %bitcast.4), calls=%async_computation.4 | async-start | bytes 262144 | tf_op jit(solution)/shard_map/all_to_all | solution.py:42
  45.1 0.5 broadcast.33
  45.6 0.7 reduce.3
  46.4 6.0 %all-to-all-done.1 = bf16[8,64,128]{2,1,0:T(8,128)(2,1)S(1)} async-done(((bf16[8,64,128]{2,1,0:T(8,128)(2,1)}), bf16[8,64,128]{2,1,0:T(8,128)(2,1)S(1)}, u32[]{:S(2)}, u32[]{:S(2)}) %all-to-all-start.1) | async-done | bytes 131104 | tf_op jit(solution)/shard_map/all_to_all | solution.py:42
  52.3 9.3 %while.10 = (s32[]{:T(128)}, f32[4,512,128]{2,1,0:T(8,128)}, s32[4]{0:T(128)S(1)}, s32[512]{0:T(512)S(1)}, bf16[512,128]{1,0:T(8,128)(2,1)S(1)}, /*index=5*/s32[]{:T(128)}, s32[1]{0:T(128)}) while((s32[]{:T(128)}, f32[4,512,128]{2,1,0:T(8,128)}, s32[4]{0:T(128)S(1)}, s32[512]{0:T(512)S(1)}, bf16[512,128]{1,0:T(8,128)(2,1)S(1)}, ...), condition=%wide.region_5.6_spmd, body=%wide.region_4.5_spmd.sunk | while | flops 67371520 | bytes 399477 | solution.py:18
  52.3 0.6 dynamic_slice.5
  53.6 1.1 fusion.26
  54.6 0.6 dynamic_slice.5
  55.9 1.1 fusion.26
  57.0 0.6 dynamic_slice.5
  58.2 1.1 fusion.26
  59.3 0.6 dynamic_slice.5
  60.5 1.1 fusion.26
  62.2 33.4 %reduce-scatter.7.cloned.1.call-done = f32[256,1024]{0,1:T(8,128)} async-done(((f32[1024,1024]{0,1:T(8,128)}), f32[256,1024]{0,1:T(8,128)}) %reduce-scatter.7.cloned.1.call-update) | async-done | bytes 1048592 | tf_op jit(solution)/shard_map/reduce_scatter | solution.py:46
  95.7 2.5 copy.17
  98.2 36.7 %all-reduce.2.cloned.1.call-done = f32[2048,128]{1,0:T(8,128)} async-done(((f32[2048,128]{1,0:T(8,128)}), f32[2048,128]{1,0:T(8,128)}) %all-reduce.2.cloned.1.call-update) | async-done | bytes 1048592 | tf_op jit(solution)/shard_map/psum | solution.py:63
  134.9 3.3 %divide_subtract_fusion = (f32[2048,128]{1,0:T(8,128)}, f32[2048,128]{1,0:T(8,128)}) fusion(f32[2048,128]{1,0:T(8,128)S(1)} %copy-done.1, f32[2048,128]{1,0:T(8,128)} %all-reduce.2.cloned.1.call-done, f32[2048,128]{1,0:T(8,128)} %param.19), kind=kLoop, calls=%fused_computation.15 | loop fusion | flops 1572864 | bytes 5242880 | tf_op jit(solution)/shard_map/sub | solution.py:65
  138.3 63.6 %reduce-scatter.11.cloned.1.call-done = f32[32,512]{1,0:T(8,128)} async-done(((f32[256,512]{1,0:T(8,128)}), f32[32,512]{1,0:T(8,128)}) %reduce-scatter.11.cloned.1.call-update) | async-done | bytes 65552 | tf_op jit(solution)/shard_map/reduce_scatter | solution.py:60
  201.8 67.0 %reduce-scatter.13.cloned.1.call-done = f32[32,1024]{1,0:T(8,128)} async-done(((f32[256,1024]{1,0:T(8,128)}), f32[32,1024]{1,0:T(8,128)}) %reduce-scatter.13.cloned.1.call-update) | async-done | bytes 131088
  (30 shorter events, 1.1 us)
Async XLA Ops:
  7.2 1.6 copy-start
  7.2 7.5 %copy-start.3 = (bf16[1024,512]{1,0:T(8,128)(2,1)S(1)}, bf16[1024,512]{1,0:T(8,128)(2,1)}, u32[]{:S(2)}) copy-start(bf16[1024,512]{1,0:T(8,128)(2,1)} %param.14) | copy-start | bytes 3145732
  7.2 54.5 %reduce-scatter.9.cloned.1.call-start = ((), (), s32[]{:S(2)}) async-start(), calls=%async_computation.7 | async-start | bytes 2621440 | tf_op jit(solution)/shard_map/reduce_scatter | solution.py:54
  14.6 81.0 %reduce-scatter.7.cloned.1.call-start = ((), (), s32[]{:S(2)}) async-start(), calls=%async_computation.6 | async-start | bytes 5242880 | tf_op jit(solution)/shard_map/reduce_scatter | solution.py:46
  27.0 0.7 copy-start.4
  27.0 0.8 copy-start.2
  27.7 107.2 %copy-start.1 = (f32[2048,128]{1,0:T(8,128)S(1)}, f32[2048,128]{1,0:T(8,128)}, u32[]{:S(2)}) copy-start(f32[2048,128]{1,0:T(8,128)} %param.18) | copy-start | bytes 3145732
  41.7 10.7 %all-to-all-start.1 = ((bf16[8,64,128]{2,1,0:T(8,128)(2,1)}), bf16[8,64,128]{2,1,0:T(8,128)(2,1)S(1)}, u32[]{:S(2)}, u32[]{:S(2)}) async-start(bf16[8,64,128]{2,1,0:T(8,128)(2,1)} %bitcast.4), calls=%async_computation.4 | async-start | bytes 262144 | tf_op jit(solution)/shard_map/all_to_all | solution.py:42
  45.0 89.9 %all-reduce.2.cloned.1.call-start = ((), (), s32[]{:S(2)}) async-start(), calls=%async_computation.9 | async-start | bytes 2097152 | tf_op jit(solution)/shard_map/psum | solution.py:63
  61.6 140.2 %reduce-scatter.11.cloned.1.call-start = ((), (), s32[]{:S(2)}) async-start(), calls=%async_computation.8 | async-start | bytes 589824 | tf_op jit(solution)/shard_map/reduce_scatter | solution.py:60
  62.2 206.6 %reduce-scatter.13.cloned.1.call-start = ((), (), s32[]{:S(2)}) async-start(), calls=%async_computation.10 | async-start | bytes 1179648
Sparse Core Ops, SparseCore 0:
  14.8 33.8 reduce-scatter.8
  51.2 44.3 reduce-scatter.6
  98.6 36.2 all-reduce.1
  138.7 63.0 reduce-scatter.10
  205.6 63.1 reduce-scatter.12
where the time goes:
time: 276 us; the launch traced here: 275 us
  waiting for transfers between devices  207 us (75%)
  matrix products  22.5 us (8%)
  between operations  13.8 us (5%)
  blocking collectives  13.7 us (5%)
  local copies, waits for them, and re-layouts  7.79 us (3%)
  other arithmetic  4.08 us (1%)
  starting transfers between devices  3.57 us (1%)
    unnamed x6, waiting for transfers between devices  67.6 us
    reduce_scatter x1, waiting for transfers between devices, on_device(): lax.psum_scatter(second_share, 'dev', scatter_dimension=0, tiled=True)  63.6 us
    psum x1, waiting for transfers between devices, on_device(): table_grad = lax.psum(local_grad, 'grp')  36.7 us
    reduce_scatter x1, waiting for transfers between devices, on_device(): lax.psum_scatter(lax.dot_general(columns, d_hidden, contract, preferred_e...  33.4 us
    all_to_all x1, blocking collectives, on_device(): lax.all_to_all(sent_ids, 'dev', split_axis=0, concat_axis=0, tiled=True)  13.7 us
    dot_general x1, matrix products, on_device(): lax.dot_general(columns, d_hidden, contract, preferred_element_type=jnp.f...  12.3 us
    all_to_all x1, waiting for transfers between devices, on_device(): lax.all_to_all(row_grads, 'dev', split_axis=0, concat_axis=0, tiled=True)  5.97 us
    dot_general x1, matrix products, on_device(): lax.dot_general(columns, out_grad, contract, preferred_element_type=jnp.f...  5.86 us
  transfers between devices with their start and end apart: 6, of which 5 were waited for; matrix products, arithmetic and copies ran while one was open for 9% of the time, Pallas kernels for 0%

commit v1 on v0

v1 whole, which is shorter than its diff:
```python
import functools

import jax
import jax.numpy as jnp
from jax import lax
from jax.experimental import pallas as pl
from jax.experimental.pallas import tpu as pltpu
from jax.sharding import PartitionSpec as P

learn_rate = 0.5
epsilon = 1e-08
MESH = pl.DeviceIdType.MESH
LANES = 128


def kernel(
    G, D,
    x_hbm, h_hbm, og_hbm, w2_hbm, rg_hbm, ids_hbm, tab_hbm, st_hbm,
    g1_ref, g2_ref, ntab_hbm, nst_hbm,
    x_v, h_v, og_v, w2_v, tab_v, st_v, dh_v, lt_v,
    eb, ib,
    cs2, cr2, xs2, xr2, kp2, zs2, zf2, zr2,
    cs1, cr1, xs1, xr1, kp1, zs1, zf1, zr1,
    lsem, cs_s, cr_s, xs_s, xr_s, zs_s, zr_s, e1s, e1r, e2s, e2r,
):
    GX, DH = G // 2, D // 2
    g, d = lax.axis_index("grp"), lax.axis_index("dev")
    gx, c = g // 2, g % 2
    dh, dl = d // 2, d % 2
    tokens = x_v.shape[0]
    R = g1_ref.shape[0]
    DR = D * R
    tile = 256
    f32, bf16 = jnp.float32, jnp.bfloat16

    def local(src, dst, i):
        return pltpu.make_async_copy(src, dst, lsem.at[i])

    loads = [
        local(h_hbm, h_v, 0),
        local(og_hbm, og_v, 1),
        local(w2_hbm, w2_v, 2),
        local(x_hbm, x_v, 3),
        local(rg_hbm.at[d], eb.at[g, d], 4),
        local(ids_hbm.at[d], ib.at[g, d], 5),
        local(tab_hbm, tab_v, 6),
        local(st_hbm, st_v, 7),
    ]
    for load in loads:
        load.start()

    peers = [(gx * 2 + (c + 1) % 2, d)]
    plane = []
    for kx in range(GX):
        for kl in range(2):
            if kx or kl:
                plane.append((kx, kl, ((gx + kx) % GX) * 2 + c, dh * 2 + (dl + kl) % 2))
    line = [(k, ((dh + k) % DH) * 2 + dl) for k in range(1, DH)]
    owners = [(k, (d + k) % D) for k in range(1, D)]
    groups = [(k, (g + k) % G) for k in range(1, G)]
    for kx, kl, pg, pd in plane:
        peers.append((pg, pd))
    for k, pd in owners:
        peers.append((g, pd))
    for k, pg in groups:
        peers.append((pg, d))
    barrier = pltpu.get_barrier_semaphore()
    for peer in peers:
        pl.semaphore_signal(barrier, inc=1, device_id=peer, device_id_type=MESH)
    pl.semaphore_wait(barrier, len(peers))

    def remote(src, dst, ss, rs, to):
        return pltpu.make_async_remote_copy(
            src_ref=src, dst_ref=dst, send_sem=ss, recv_sem=rs, device_id=to, device_id_type=MESH
        )

    pending = []

    def send(*args):
        copy = remote(*args)
        copy.start()
        pending.append(copy)

    for k, pd in owners:
        send(rg_hbm.at[pd], eb.at[g, d], e1s.at[0, k], e1r.at[0, k], (g, pd))
        send(ids_hbm.at[pd], ib.at[g, d], e1s.at[1, k], e1r.at[1, k], (g, pd))

    other = (gx * 2 + (c + 1) % 2, d)

    def transpose(src, target_group, relu):
        cols = pl.ds(pl.multiple_of(target_group * DR, DR), DR)

        def body(t, _):
            rows = pl.ds(pl.multiple_of(t * tile, tile), tile)
            block = src[rows, cols]
            if relu:
                block = jnp.maximum(block, jnp.zeros_like(block))
            lt_v[:, rows] = block.T
            return 0

        lax.fori_loop(0, tokens // tile, body, 0)

    def product(rhs, out_tile):
        width = rhs.shape[1]

        def body(n, _):
            ns = pl.ds(pl.multiple_of(n * tile, tile), tile)
            out_tile(ns, jnp.dot(lt_v[...], rhs[:, ns], preferred_element_type=f32))
            return 0

        lax.fori_loop(0, width // tile, body, 0)

    order = [1 % GX] + [k for k in range(GX) if k != 1 % GX]

    def away(a, src, relu, rhs, cs, cr):
        for kx in order:
            transpose(src, ((gx + kx) % GX) * 2 + (c + 1) % 2, relu)

            def put(ns, value, kx=kx):
                cs[kx, :, ns] = value

            product(rhs, put)
            send(cs.at[kx], cr.at[kx], cs_s.at[a, kx], cr_s.at[a, kx], other)

    def home(a, src, relu, rhs, cr, xs, xr, kp):
        for kx in order:
            transpose(src, ((gx + kx) % GX) * 2 + c, relu)
            remote(cr.at[kx], cr.at[kx], cs_s.at[a, kx], cr_s.at[a, kx], other).wait_recv()

            def put(ns, value, kx=kx):
                value = value + cr[kx, :, ns]
                for b in range(DH):
                    for l in range(2):
                        at = (b * 2 + l) * R
                        piece = value[at : at + R]
                        xs[kx, l, b, :, ns] = piece.astype(bf16)
                        if kx == 0:
                            kp[l, b, :, ns] = piece

            product(rhs, put)
            for px, kl, pg, pd in plane[::-1]:
                if px == kx:
                    i = px * 2 + kl
                    send(xs.at[kx, (dl + kl) % 2], xr.at[i], xs_s.at[a, i], xr_s.at[a, i], (pg, pd))

    def along(a, xr, kp, zs, zf, zr):
        for px, kl, pg, pd in plane:
            i = px * 2 + kl
            remote(xr.at[i], xr.at[i], xs_s.at[a, i], xr_s.at[a, i], (pg, pd)).wait_recv()
        for b in range(DH):
            value = kp[dl, b]
            for px, kl, pg, pd in plane:
                value = value + xr[px * 2 + kl, b].astype(f32)
            zf[b] = value
            zs[b] = value.astype(bf16)
        for k, pd in line[::-1]:
            send(zs.at[(dh + k) % DH], zr.at[k], zs_s.at[a, k], zr_s.at[a, k], (g, pd))

    def finish(a, zf, zr, out):
        value = zf[dh]
        for k, pd in line:
            remote(zr.at[k], zr.at[k], zs_s.at[a, k], zr_s.at[a, k], (g, pd)).wait_recv()
            value = value + zr[k].astype(f32)
        out[...] = value

    loads[0].wait()
    loads[1].wait()
    away(0, h_v, True, og_v, cs2, cr2)
    home(0, h_v, True, og_v, cr2, xs2, xr2, kp2)

    loads[4].wait()
    loads[5].wait()
    for k, pd in owners:
        src = (d + D - k) % D
        remote(eb.at[g, src], eb.at[g, src], e1s.at[0, k], e1r.at[0, k], (g, pd)).wait_recv()
        remote(ib.at[g, src], ib.at[g, src], e1s.at[1, k], e1r.at[1, k], (g, pd)).wait_recv()
    for k, pg in groups:
        send(eb.at[g], eb.at[g], e2s.at[0, k], e2r.at[0, k], (pg, d))
        send(ib.at[g], ib.at[g], e2s.at[1, k], e2r.at[1, k], (pg, d))

    loads[2].wait()

    def back_tile(t, _):
        rows = pl.ds(pl.multiple_of(t * tile, tile), tile)
        back = lax.dot_general(
            og_v[rows, :], w2_v[...], (((1,), (1,)), ((), ())), preferred_element_type=f32
        )
        keep = h_v[rows, :].astype(f32) > 0
        dh_v[rows, :] = jnp.where(keep, back, jnp.zeros_like(back)).astype(bf16)
        return 0

    lax.fori_loop(0, tokens // tile, back_tile, 0)

    loads[3].wait()
    away(1, x_v, False, dh_v, cs1, cr1)
    home(1, x_v, False, dh_v, cr1, xs1, xr1, kp1)
    along(0, xr2, kp2, zs2, zf2, zr2)

    loads[6].wait()
    loads[7].wait()
    for k, pg in groups:
        src = (g + G - k) % G
        remote(eb.at[src], eb.at[src], e2s.at[0, k], e2r.at[0, k], (pg, d)).wait_recv()
        remote(ib.at[src], ib.at[src], e2s.at[1, k], e2r.at[1, k], (pg, d)).wait_recv()
    cap = eb.shape[2]
    pack = LANES // cap
    owned = tab_v.shape[0]

    def owned_tile(t, _):
        start = pl.multiple_of(t * tile, tile)
        rows = pl.ds(start, tile)
        wanted = start + lax.broadcasted_iota(jnp.int32, (tile, LANES), 0)
        total = jnp.zeros((tile, eb.shape[3]), f32)
        for q in range(G):
            parts = []
            for s in range(0, D, pack):
                ids = ib[q, s]
                for e in range(1, pack):
                    ids = jnp.maximum(ids, ib[q, s + e])
                hit = wanted == ids[0:1, :]
                parts.append(jnp.where(hit, 1.0, 0.0).astype(bf16))
            onehot = jnp.concatenate(parts, axis=1)
            total = total + jnp.dot(
                onehot, eb[q].reshape(D * cap, eb.shape[3]), preferred_element_type=f32
            )
        state = st_v[rows, :] + total * total
        st_v[rows, :] = state
        tab_v[rows, :] = tab_v[rows, :] - learn_rate * total / (jnp.sqrt(state) + epsilon)
        return 0

    lax.fori_loop(0, owned // tile, owned_tile, 0)
    stores = [local(tab_v, ntab_hbm, 0), local(st_v, nst_hbm, 1)]
    for store in stores:
        store.start()

    finish(0, zf2, zr2, g2_ref)
    along(1, xr1, kp1, zs1, zf1, zr1)
    finish(1, zf1, zr1, g1_ref)
    for copy in pending:
        copy.wait_send()
    for store in stores:
        store.wait()


def solution(mesh):
    G, D = mesh.shape["grp"], mesh.shape["dev"]

    def on_device(
        layer_input, hidden_pre, out_grad, second_weight,
        row_grads, row_ids, block_counts, emb_table, adagrad_state,
    ):
        T, IN = layer_input.shape
        HID, OUT = second_weight.shape
        E = row_grads.shape[1]
        cap = row_grads.shape[0] // D
        owned = emb_table.shape[0]
        GX, DH = G // 2, D // 2
        pack = LANES // cap
        R1, R2 = IN // (G * D), HID // (G * D)
        lane = jnp.arange(LANES, dtype=jnp.int32)
        mine = lax.axis_index("dev") % pack
        usable = (lane[None, :] % cap < block_counts[:, None]) & (lane[None, :] // cap == mine)
        ids = jnp.where(usable, jnp.tile(row_ids.reshape(D, cap), (1, pack)), -1)
        ids = jnp.broadcast_to(ids[:, None, :], (D, 8, LANES))
        f32, bf16 = jnp.float32, jnp.bfloat16

        def stages(R, N):
            return [
                pltpu.VMEM((GX, D * R, N), f32),
                pltpu.VMEM((GX, D * R, N), f32),
                pltpu.VMEM((GX, 2, DH, R, N), bf16),
                pltpu.VMEM((GX * 2, DH, R, N), bf16),
                pltpu.VMEM((2, DH, R, N), f32),
                pltpu.VMEM((DH, R, N), bf16),
                pltpu.VMEM((DH, R, N), f32),
                pltpu.VMEM((DH, R, N), bf16),
            ]

        hbm = pl.BlockSpec(memory_space=pltpu.HBM)
        vmem = pl.BlockSpec(memory_space=pltpu.VMEM)
        dma = pltpu.SemaphoreType.DMA
        return pl.pallas_call(
            functools.partial(kernel, G, D),
            out_shape=[
                jax.ShapeDtypeStruct((R1, HID), f32),
                jax.ShapeDtypeStruct((R2, OUT), f32),
                jax.ShapeDtypeStruct(emb_table.shape, f32),
                jax.ShapeDtypeStruct(adagrad_state.shape, f32),
            ],
            in_specs=[hbm] * 8,
            out_specs=[vmem, vmem, hbm, hbm],
            scratch_shapes=[
                pltpu.VMEM((T, IN), bf16),
                pltpu.VMEM((T, HID), bf16),
                pltpu.VMEM((T, OUT), bf16),
                pltpu.VMEM((HID, OUT), bf16),
                pltpu.VMEM((owned, E), f32),
                pltpu.VMEM((owned, E), f32),
                pltpu.VMEM((T, HID), bf16),
                pltpu.VMEM((D * R1, T), bf16),
                pltpu.VMEM((G, D, cap, E), bf16),
                pltpu.VMEM((G, D, 8, LANES), jnp.int32),
                *stages(R2, OUT),
                *stages(R1, HID),
                dma((8,)),
                dma((2, GX)), dma((2, GX)),
                dma((2, GX * 2)), dma((2, GX * 2)),
                dma((2, DH)), dma((2, DH)),
                dma((2, D)), dma((2, D)),
                dma((2, G)), dma((2, G)),
            ],
            compiler_params=pltpu.CompilerParams(
                collective_id=0, has_side_effects=True, vmem_limit_bytes=60 * 1024 * 1024
            ),
        )(
            layer_input, hidden_pre, out_grad, second_weight,
            row_grads.reshape(D, cap, E), ids, emb_table, adagrad_state,
        )

    return jax.shard_map(
        on_device,
        mesh=mesh,
        in_specs=(
            P(("grp", "dev"), None),
            P(("grp", "dev"), None),
            P(("grp", "dev"), None),
            P(),
            P(("grp", "dev"), None),
            P(("grp", "dev")),
            P(("grp", "dev")),
            P("dev", None),
            P("dev", None),
        ),
        out_specs=(P(("grp", "dev"), None), P(("grp", "dev"), None), P("dev", None), P("dev", None)),
        check_vma=False,
    )
```

time: 276 us -> 58.5 us (0.21)
  waiting for transfers between devices: 207 us -> 0 us
  Pallas kernels: 0 us -> 47.8 us
  matrix products: 22.5 us -> 0 us
  blocking collectives: 13.7 us -> 0 us
  between operations: 13.8 us -> 0.67 us
  starting transfers between devices: 3.57 us -> 0 us
  other arithmetic: 4.08 us -> 0.74 us
    reduce_scatter x3 -> x0, waiting for transfers between devices: 97 us -> none  [the longest x1 63.6 us: on_device(): lax.psum_scatter(second_share, 'dev', scatter_dimension=0, tiled=True)]
    unnamed x6 -> x0, waiting for transfers between devices: 67.6 us -> none
    pallas_call x0 -> x1, Pallas kernels: none -> 47.8 us  [on_device(): pl.pallas_call(functools.partial(kernel, G, D), out_shape=[jax.ShapeDtype...]
    psum x1 -> x0, waiting for transfers between devices: 36.7 us -> none  [on_device(): table_grad = lax.psum(local_grad, 'grp')]
    dot_general x6 -> x0, matrix products: 22.5 us -> none  [the longest x1 12.3 us: on_device(): lax.dot_general(columns, d_hidden, contract, preferred_element_type=jnp.f...]
    all_to_all x1 -> x0, blocking collectives: 13.7 us -> none  [on_device(): lax.all_to_all(sent_ids, 'dev', split_axis=0, concat_axis=0, tiled=True)]
    all_to_all x1 -> x0, waiting for transfers between devices: 5.97 us -> none  [on_device(): lax.all_to_all(row_grads, 'dev', split_axis=0, concat_axis=0, tiled=True)]
    all_to_all x1 -> x0, starting transfers between devices: 3.37 us -> none  [on_device(): lax.all_to_all(row_grads, 'dev', split_axis=0, concat_axis=0, tiled=True)]
  transfers between devices with their start and end apart: 6 -> 0, of which waited for: 5 -> 0; matrix products, arithmetic and copies ran while one was open for 9% -> 0% of each run, Pallas kernels for 0% -> 0%
where the time goes in v1:
time: 58.5 us; the launch traced here: 58.2 us
  Pallas kernels  47.8 us (82%)
  local copies, waits for them, and re-layouts  9.03 us (15%)
  other arithmetic  0.74 us (1%)
  between operations  0.67 us (1%)
    pallas_call x1, Pallas kernels, on_device(): pl.pallas_call(functools.partial(kernel, G, D), out_shape=[jax.ShapeDtype...  47.8 us
    unnamed x4, local copies, waits for them, and re-layouts  7.56 us

profile of v1, /device:TPU:0, one launch (start us, length us, event | category | flops | bytes accessed | tf_op | source)
XLA Modules:
  0.0 58.2 jit_solution(16909843442724918418)
XLA Ops:
  0.7 0.8 %tile.10 = s32[8,64]{1,0:T(8,128)S(1)} reshape(s32[512]{0:T(512)} %param.14) | data formatting | bytes 4096 | tf_op jit(solution)/shard_map/tile | solution.py:263
  1.4 0.1 tile.12
  1.5 0.7 %and_select_fusion = s32[8,128]{1,0:T(8,128)S(1)} fusion(s32[8,128]{1,0:T(8,128)S(1)} %tile.12, s32[128]{0:T(128)S(1)} %and_select_fusion.2, s32[8]{0:T(128)} %param.15, pred[128]{0:T(512)(128)(4,1)S(1)} %fusion), kind=kLoop, calls=%fused_computation | loop fusion | flops 3072 | bytes 8864 | tf_op jit(solution)/shard_map/jit(_where)/select_n | solution.py:263
  2.2 0.6 %broadcast_in_dim.7.ids_hbm = s32[8,8,128]{2,1,0:T(8,128)} broadcast(s32[8,128]{1,0:T(8,128)S(1)} %and_select_fusion), dimensions={0,2} | broadcast | bytes 36864 | tf_op jit(solution)/shard_map/broadcast_in_dim | solution.py:264
  2.9 47.8 %shard_map.120 = (f32[32,1024]{1,0:T(8,128)}, f32[32,512]{1,0:T(8,128)}, f32[2048,128]{1,0:T(8,128)}, f32[2048,128]{1,0:T(8,128)}) custom-call(bf16[2048,1024]{1,0:T(8,128)(2,1)} %x_hbm.1, bf16[2048,1024]{1,0:T(8,128)(2,1)} %h_hbm.1, bf16[2048,512]{1,0:T(8,128)(2,1)} %og_hbm.1, bf16[1024,512]{1,0:T(8,128)(2,1)} %w2_hbm.1, bf16[8,64,128]{2,1,0:T(8,128)(2,1)} %bitcast.1, ...), custom_call_target="tpu_custom_call" | custom-call | tf_op jit(solution)/shard_map/pallas_call | solution.py:282
  50.7 1.6 %copy.17 = f32[32,1024]{1,0:T(8,128)} copy(f32[32,1024]{1,0:T(8,128)} %get-tuple-element.8) | data formatting | bytes 262144
  52.2 1.5 %copy.18 = f32[32,512]{1,0:T(8,128)} copy(f32[32,512]{1,0:T(8,128)} %get-tuple-element.9) | data formatting | bytes 131072
  53.7 2.3 %copy.19 = f32[2048,128]{1,0:T(8,128)} copy(f32[2048,128]{1,0:T(8,128)} %get-tuple-element.10) | data formatting | bytes 2097152
  56.0 2.3 %copy.20 = f32[2048,128]{1,0:T(8,128)} copy(f32[2048,128]{1,0:T(8,128)} %get-tuple-element.11) | data formatting | bytes 2097152
  (3 shorter events, 0.0 us)

commit v2 on v1

--- a/solution.py
+++ b/solution.py
@@ -15,9 +15,9 @@
 
 def kernel(
     G, D,
-    x_hbm, h_hbm, og_hbm, w2_hbm, rg_hbm, ids_hbm, tab_hbm, st_hbm,
-    g1_ref, g2_ref, ntab_hbm, nst_hbm,
-    x_v, h_v, og_v, w2_v, tab_v, st_v, dh_v, lt_v,
+    x_hbm, h_hbm, og_hbm, w2_hbm, rg_hbm, ids_hbm,
+    g1_ref, g2_ref, tg_hbm,
+    x_v, h_v, og_v, w2_v, wt_v, tg_v, dh_v, lt_v,
     eb, ib,
     cs2, cr2, xs2, xr2, kp2, zs2, zf2, zr2,
     cs1, cr1, xs1, xr1, kp1, zs1, zf1, zr1,
@@ -31,20 +31,19 @@
     R = g1_ref.shape[0]
     DR = D * R
     tile = 256
+    wide = min(tokens, 1024)
     f32, bf16 = jnp.float32, jnp.bfloat16
 
     def local(src, dst, i):
         return pltpu.make_async_copy(src, dst, lsem.at[i])
 
     loads = [
-        local(h_hbm, h_v, 0),
-        local(og_hbm, og_v, 1),
-        local(w2_hbm, w2_v, 2),
+        local(w2_hbm, w2_v, 0),
+        local(h_hbm, h_v, 1),
+        local(og_hbm, og_v, 2),
         local(x_hbm, x_v, 3),
         local(rg_hbm.at[d], eb.at[g, d], 4),
         local(ids_hbm.at[d], ib.at[g, d], 5),
-        local(tab_hbm, tab_v, 6),
-        local(st_hbm, st_v, 7),
     ]
     for load in loads:
         load.start()
@@ -90,15 +89,11 @@
     def transpose(src, target_group, relu):
         cols = pl.ds(pl.multiple_of(target_group * DR, DR), DR)
 
-        def body(t, _):
-            rows = pl.ds(pl.multiple_of(t * tile, tile), tile)
-            block = src[rows, cols]
+        for t in range(0, tokens, wide):
+            block = src[t : t + wide, cols]
             if relu:
                 block = jnp.maximum(block, jnp.zeros_like(block))
-            lt_v[:, rows] = block.T
-            return 0
-
-        lax.fori_loop(0, tokens // tile, body, 0)
+            lt_v[:, t : t + wide] = block.T
 
     def product(rhs, out_tile):
         width = rhs.shape[1]
@@ -112,8 +107,8 @@
 
     order = [1 % GX] + [k for k in range(GX) if k != 1 % GX]
 
-    def away(a, src, relu, rhs, cs, cr):
-        for kx in order:
+    def away(only, a, src, relu, rhs, cs, cr):
+        for kx in (only,):
             transpose(src, ((gx + kx) % GX) * 2 + (c + 1) % 2, relu)
 
             def put(ns, value, kx=kx):
@@ -122,8 +117,8 @@
             product(rhs, put)
             send(cs.at[kx], cr.at[kx], cs_s.at[a, kx], cr_s.at[a, kx], other)
 
-    def home(a, src, relu, rhs, cr, xs, xr, kp):
-        for kx in order:
+    def home(only, a, src, relu, rhs, cr, xs, xr, kp):
+        for kx in (only,):
             transpose(src, ((gx + kx) % GX) * 2 + c, relu)
             remote(cr.at[kx], cr.at[kx], cs_s.at[a, kx], cr_s.at[a, kx], other).wait_recv()
 
@@ -164,27 +159,30 @@
         out[...] = value
 
     loads[0].wait()
+    for n in range(0, w2_v.shape[0], tile):
+        wt_v[:, n : n + tile] = w2_v[n : n + tile, :].T
     loads[1].wait()
-    away(0, h_v, True, og_v, cs2, cr2)
-    home(0, h_v, True, og_v, cr2, xs2, xr2, kp2)
-
-    loads[4].wait()
-    loads[5].wait()
-    for k, pd in owners:
-        src = (d + D - k) % D
-        remote(eb.at[g, src], eb.at[g, src], e1s.at[0, k], e1r.at[0, k], (g, pd)).wait_recv()
-        remote(ib.at[g, src], ib.at[g, src], e1s.at[1, k], e1r.at[1, k], (g, pd)).wait_recv()
-    for k, pg in groups:
-        send(eb.at[g], eb.at[g], e2s.at[0, k], e2r.at[0, k], (pg, d))
-        send(ib.at[g], ib.at[g], e2s.at[1, k], e2r.at[1, k], (pg, d))
-
     loads[2].wait()
+    def hand_over():
+        loads[4].wait()
+        loads[5].wait()
+        for k, pd in owners:
+            src = (d + D - k) % D
+            remote(eb.at[g, src], eb.at[g, src], e1s.at[0, k], e1r.at[0, k], (g, pd)).wait_recv()
+            remote(ib.at[g, src], ib.at[g, src], e1s.at[1, k], e1r.at[1, k], (g, pd)).wait_recv()
+        for k, pg in groups:
+            send(eb.at[g], eb.at[g], e2s.at[0, k], e2r.at[0, k], (pg, d))
+            send(ib.at[g], ib.at[g], e2s.at[1, k], e2r.at[1, k], (pg, d))
+
+    for only in order:
+        away(only, 0, h_v, True, og_v, cs2, cr2)
+    for only in order:
+        home(only, 0, h_v, True, og_v, cr2, xs2, xr2, kp2)
+    hand_over()
 
     def back_tile(t, _):
         rows = pl.ds(pl.multiple_of(t * tile, tile), tile)
-        back = lax.dot_general(
-            og_v[rows, :], w2_v[...], (((1,), (1,)), ((), ())), preferred_element_type=f32
-        )
+        back = jnp.dot(og_v[rows, :], wt_v[...], preferred_element_type=f32)
         keep = h_v[rows, :].astype(f32) > 0
         dh_v[rows, :] = jnp.where(keep, back, jnp.zeros_like(back)).astype(bf16)
         return 0
@@ -192,19 +190,19 @@
     lax.fori_loop(0, tokens // tile, back_tile, 0)
 
     loads[3].wait()
-    away(1, x_v, False, dh_v, cs1, cr1)
-    home(1, x_v, False, dh_v, cr1, xs1, xr1, kp1)
+    for only in order:
+        away(only, 1, x_v, False, dh_v, cs1, cr1)
+    for only in order:
+        home(only, 1, x_v, False, dh_v, cr1, xs1, xr1, kp1)
     along(0, xr2, kp2, zs2, zf2, zr2)
 
-    loads[6].wait()
-    loads[7].wait()
     for k, pg in groups:
         src = (g + G - k) % G
         remote(eb.at[src], eb.at[src], e2s.at[0, k], e2r.at[0, k], (pg, d)).wait_recv()
         remote(ib.at[src], ib.at[src], e2s.at[1, k], e2r.at[1, k], (pg, d)).wait_recv()
     cap = eb.shape[2]
     pack = LANES // cap
-    owned = tab_v.shape[0]
+    owned = tg_v.shape[0]
 
     def owned_tile(t, _):
         start = pl.multiple_of(t * tile, tile)
@@ -223,23 +221,30 @@
             total = total + jnp.dot(
                 onehot, eb[q].reshape(D * cap, eb.shape[3]), preferred_element_type=f32
             )
-        state = st_v[rows, :] + total * total
-        st_v[rows, :] = state
-        tab_v[rows, :] = tab_v[rows, :] - learn_rate * total / (jnp.sqrt(state) + epsilon)
+        tg_v[rows, :] = total
         return 0
 
     lax.fori_loop(0, owned // tile, owned_tile, 0)
-    stores = [local(tab_v, ntab_hbm, 0), local(st_v, nst_hbm, 1)]
+    stores = [local(tg_v, tg_hbm, 0)]
     for store in stores:
         store.start()
 
+    along(1, xr1, kp1, zs1, zf1, zr1)
     finish(0, zf2, zr2, g2_ref)
-    along(1, xr1, kp1, zs1, zf1, zr1)
     finish(1, zf1, zr1, g1_ref)
     for copy in pending:
         copy.wait_send()
     for store in stores:
         store.wait()
+
+
+def update(g1_in, g2_in, sum_in, tab_in, st_in, g1_out, g2_out, tab_out, st_out):
+    g1_out[...] = g1_in[...]
+    g2_out[...] = g2_in[...]
+    total = sum_in[...]
+    state = st_in[...] + total * total
+    st_out[...] = state
+    tab_out[...] = tab_in[...] - learn_rate * total / (jnp.sqrt(state) + epsilon)
 
 
 def solution(mesh):
@@ -261,7 +266,7 @@
         mine = lax.axis_index("dev") % pack
         usable = (lane[None, :] % cap < block_counts[:, None]) & (lane[None, :] // cap == mine)
         ids = jnp.where(usable, jnp.tile(row_ids.reshape(D, cap), (1, pack)), -1)
-        ids = jnp.broadcast_to(ids[:, None, :], (D, 8, LANES))
+        ids = ids[:, None, :]
         f32, bf16 = jnp.float32, jnp.bfloat16
 
         def stages(R, N):
@@ -279,27 +284,26 @@
         hbm = pl.BlockSpec(memory_space=pltpu.HBM)
         vmem = pl.BlockSpec(memory_space=pltpu.VMEM)
         dma = pltpu.SemaphoreType.DMA
-        return pl.pallas_call(
+        g1, g2, summed = pl.pallas_call(
             functools.partial(kernel, G, D),
             out_shape=[
                 jax.ShapeDtypeStruct((R1, HID), f32),
                 jax.ShapeDtypeStruct((R2, OUT), f32),
                 jax.ShapeDtypeStruct(emb_table.shape, f32),
-                jax.ShapeDtypeStruct(adagrad_state.shape, f32),
             ],
-            in_specs=[hbm] * 8,
-            out_specs=[vmem, vmem, hbm, hbm],
+            in_specs=[hbm] * 6,
+            out_specs=[vmem, vmem, hbm],
             scratch_shapes=[
                 pltpu.VMEM((T, IN), bf16),
                 pltpu.VMEM((T, HID), bf16),
                 pltpu.VMEM((T, OUT), bf16),
                 pltpu.VMEM((HID, OUT), bf16),
-                pltpu.VMEM((owned, E), f32),
+                pltpu.VMEM((OUT, HID), bf16),
                 pltpu.VMEM((owned, E), f32),
                 pltpu.VMEM((T, HID), bf16),
                 pltpu.VMEM((D * R1, T), bf16),
                 pltpu.VMEM((G, D, cap, E), bf16),
-                pltpu.VMEM((G, D, 8, LANES), jnp.int32),
+                pltpu.VMEM((G, D, 1, LANES), jnp.int32),
                 *stages(R2, OUT),
                 *stages(R1, HID),
                 dma((8,)),
@@ -314,8 +318,24 @@
             ),
         )(
             layer_input, hidden_pre, out_grad, second_weight,
-            row_grads.reshape(D, cap, E), ids, emb_table, adagrad_state,
+            row_grads.reshape(D, cap, E), ids,
         )
+        steps = 4
+        rows = pl.BlockSpec((owned // steps, E), lambda i: (i, 0))
+        part1 = pl.BlockSpec((R1, HID // steps), lambda i: (0, i))
+        part2 = pl.BlockSpec((R2, OUT // steps), lambda i: (0, i))
+        return pl.pallas_call(
+            update,
+            grid=(steps,),
+            out_shape=[
+                jax.ShapeDtypeStruct((R1, HID), f32),
+                jax.ShapeDtypeStruct((R2, OUT), f32),
+                jax.ShapeDtypeStruct(emb_table.shape, f32),
+                jax.ShapeDtypeStruct(adagrad_state.shape, f32),
+            ],
+            in_specs=[part1, part2, rows, rows, rows],
+            out_specs=[part1, part2, rows, rows],
+        )(g1, g2, summed, emb_table, adagrad_state)
 
     return jax.shard_map(
         on_device,

time: 58.5 us -> 52.8 us (0.903)
  local copies, waits for them, and re-layouts: 9.03 us -> 0.85 us
  Pallas kernels: 47.8 us -> 49.7 us
  other arithmetic: 0.74 us -> 1.33 us
    unnamed x4 -> x0, local copies, waits for them, and re-layouts: 7.56 us -> none
    pallas_call x0 -> x1, Pallas kernels: none -> 4.09 us  [on_device(): pl.pallas_call(update, grid=(steps,), out_shape=[jax.ShapeDtypeStruct((R1...]
    pallas_call x1, Pallas kernels: 47.8 us -> 45.6 us  [on_device(): pl.pallas_call(functools.partial(kernel, G, D), out_shape=[jax.ShapeDtype...]
    broadcast_in_dim x1 -> x0, local copies, waits for them, and re-layouts: 0.62 us -> none  [on_device(): ids = jnp.broadcast_to(ids[:, None, :], (D, 8, LANES))]
    select_n x1, other arithmetic: 0.73 us -> 1.32 us  [on_device(): ids = jnp.where(usable, jnp.tile(row_ids.reshape(D, cap), (1, pack)), -1)]
where the time goes in v2:
time: 52.8 us; the launch traced here: 52.5 us
  Pallas kernels  49.7 us (94%)
  other arithmetic  1.33 us (3%)
  local copies, waits for them, and re-layouts  0.85 us (2%)
  between operations  0.66 us (1%)
    pallas_call x1, Pallas kernels, on_device(): pl.pallas_call(functools.partial(kernel, G, D), out_shape=[jax.ShapeDtype...  45.6 us
    pallas_call x1, Pallas kernels, on_device(): pl.pallas_call(update, grid=(steps,), out_shape=[jax.ShapeDtypeStruct((R1...  4.09 us
    select_n x1, other arithmetic, on_device(): ids = jnp.where(usable, jnp.tile(row_ids.reshape(D, cap), (1, pack)), -1)  1.32 us

profile of v2, /device:TPU:0, one launch (start us, length us, event | category | flops | bytes accessed | tf_op | source)
XLA Modules:
  0.0 52.5 jit_solution(6414715930289742742)
XLA Ops:
  0.7 0.8 %tile.10 = s32[8,64]{1,0:T(8,128)S(1)} reshape(s32[512]{0:T(512)} %param.14) | data formatting | bytes 4096 | tf_op jit(solution)/shard_map/tile | solution.py:268
  1.4 0.1 tile.12
  1.5 1.3 %and_select_fusion.ids_hbm = s32[8,1,128]{2,1,0:T(1,128)} fusion(s32[8,1,128]{2,1,0:T(1,128)S(1)} %tile.12, pred[128]{0:T(512)(128)(4,1)S(1)} %fusion, s32[128]{0:T(128)S(1)} %and_select_fusion.2, s32[8]{0:T(128)} %param.15), kind=kLoop, calls=%fused_computation | loop fusion | flops 3072 | bytes 8864 | tf_op jit(solution)/shard_map/jit(_where)/select_n | solution.py:268
  2.8 45.6 %shard_map.120 = (f32[32,1024]{1,0:T(8,128)}, f32[32,512]{1,0:T(8,128)}, f32[2048,128]{1,0:T(8,128)}) custom-call(bf16[2048,1024]{1,0:T(8,128)(2,1)} %x_hbm.1, bf16[2048,1024]{1,0:T(8,128)(2,1)} %h_hbm.1, bf16[2048,512]{1,0:T(8,128)(2,1)} %og_hbm.1, bf16[1024,512]{1,0:T(8,128)(2,1)} %w2_hbm.1, bf16[8,64,128]{2,1,0:T(8,128)(2,1)} %bitcast.1, ...), custom_call_target="tpu_custom_call" | custom-call | tf_op jit(solution)/shard_map/pallas_call | solution.py:287
  48.5 4.1 %shard_map.121 = (f32[32,1024]{1,0:T(8,128)}, f32[32,512]{1,0:T(8,128)}, f32[2048,128]{1,0:T(8,128)}, f32[2048,128]{1,0:T(8,128)}) custom-call(f32[32,1024]{1,0:T(8,128)} %get-tuple-element.7.g1_in, f32[32,512]{1,0:T(8,128)} %get-tuple-element.8.g2_in, f32[2048,128]{1,0:T(8,128)} %get-tuple-element.9.sum_in, f32[2048,128]{1,0:T(8,128)} %tab_in.1, ...), custom_call_target="tpu_custom_call" | custom-call | tf_op jit(solution)/shard_map/pallas_call | solution.py:327
  (3 shorter events, 0.0 us)
